TPU v7x, 32 devices: a whole 2x2x4 slice. The times are simulated.
32 devices in a mesh: dp: 8 (over y, x, core), tensor: 4 (over z).
Axes of the slice: x: 2, y: 2, z: 4, core: 2. Of those that a mesh axis runs over, the one named last changes fastest.
Arguments:
- images: bfloat16 [32, 320, 1024], P('dp', None, 'tensor'), may hold values from -6 to 6
- lengths: int32 [32], P('dp'), may hold values from 224 to 320, as said below
- cotangent: bfloat16 [32, 320, 1024], P('dp', None, 'tensor'), may hold values from -6 to 6
- norm1_gain: float32 [1024], replicated, may hold values from 0.5 to 1.5
- norm1_shift: float32 [1024], replicated, may hold values from -1.75 to 1.75
- w_qkv: bfloat16 [1024, 3, 1024], P(None, None, 'tensor'), may hold values from -0.1875 to 0.1875
- qv_bias: float32 [2, 1024], P(None, 'tensor'), may hold values from -3 to 3
- w_proj: bfloat16 [1024, 1024], P('tensor'), may hold values from -1.5 to 1.5
- proj_bias: float32 [1024], replicated, may hold values from -3 to 3
- norm2_gain: float32 [1024], replicated, may hold values from 0.5 to 1.5
- norm2_shift: float32 [1024], replicated, may hold values from -1.75 to 1.75
- w_fc1: bfloat16 [1024, 4096], P(None, 'tensor'), may hold values from -0.1875 to 0.1875
- fc1_bias: float32 [4096], P('tensor'), may hold values from -3 to 3
- w_fc2: bfloat16 [4096, 1024], P('tensor'), may hold values from -0.09375 to 0.09375
- fc2_bias: float32 [1024], replicated, may hold values from -3 to 3
Outputs:
- output: bfloat16 [32, 320, 1024], P('dp', None, 'tensor')
- input_grad: bfloat16 [32, 320, 1024], P('dp', None, 'tensor')
- grad_norm1_gain: float32 [1024], replicated
- grad_norm1_shift: float32 [1024], replicated
- grad_w_qkv: float32 [1024, 3, 1024], P(None, None, 'tensor')
- grad_qv_bias: float32 [2, 1024], P(None, 'tensor')
- grad_w_proj: float32 [1024, 1024], P('tensor')
- grad_proj_bias: float32 [1024], replicated
- grad_norm2_gain: float32 [1024], replicated
- grad_norm2_shift: float32 [1024], replicated
- grad_w_fc1: float32 [1024, 4096], P(None, 'tensor')
- grad_fc1_bias: float32 [4096], P('tensor')
- grad_w_fc2: float32 [4096, 1024], P('tensor')
- grad_fc2_bias: float32 [1024], replicated
Inputs may be any that keep to these rules, and one draw needn't show every extreme that they name: lengths[i] is the number of valid slots of image i, which come first; some image has all 320 slots valid in every draw.
All inputs are finite; a program needn't handle non-finite values.
Results may differ from a plain program's by a relative error of at most 0.02.
Values may be sent and summed in bfloat16 or wider, within the bound.
A program may use at most 192 MiB of HBM per device.

v0:
```python
import jax
import jax.numpy as jnp
from jax import lax
from jax.sharding import PartitionSpec as P

HEAD_DIM = 64
EPS = 1e-06
MASKED = -1e30


def norm_rows(values, gain_row, shift_row):
    row_mean = jnp.mean(values, axis=-1, keepdims=True)
    centered = values - row_mean
    spread = jnp.mean(centered * centered, axis=-1, keepdims=True)
    inverse = lax.rsqrt(spread + EPS)
    unit_rows = centered * inverse
    return (unit_rows * gain_row + shift_row, unit_rows, inverse)


def norm_back(gradient, unit_rows, inverse, gain_row):
    scaled = gradient * gain_row
    first_mean = jnp.mean(scaled, axis=-1, keepdims=True)
    cross_mean = jnp.mean(scaled * unit_rows, axis=-1, keepdims=True)
    return inverse * (scaled - first_mean - unit_rows * cross_mean)


def scores_of(queries, key_heads, key_mask, score_scale):
    raw_scores = (
        jnp.einsum("bqhe,bkhe->bhqk", queries, key_heads, preferred_element_type=jnp.float32)
        * score_scale
    )
    return jnp.where(key_mask, raw_scores, MASKED)


def exact_gelu(values):
    return jax.nn.gelu(values, approximate=False)


def per_device(
    images,
    lengths,
    cotangent,
    norm1_gain,
    norm1_shift,
    w_qkv,
    qv_bias,
    w_proj,
    proj_bias,
    norm2_gain,
    norm2_shift,
    w_fc1,
    fc1_bias,
    w_fc2,
    fc2_bias,
):
    images_here, slot_count, col_count = images.shape
    model_width = w_qkv.shape[0]
    local_width = w_qkv.shape[2]
    heads_here = local_width // HEAD_DIM
    row_count = images_here * slot_count
    score_scale = HEAD_DIM ** (-0.5)
    first_col = lax.axis_index("tensor") * col_count
    full_images, full_cot = (
        lax.all_gather(images, "tensor", axis=2, tiled=True),
        lax.all_gather(cotangent, "tensor", axis=2, tiled=True),
    )
    slot_ids = jnp.arange(slot_count, dtype=jnp.int32)
    valid_slots = (slot_ids[None, :] < lengths[:, None]).astype(jnp.float32)
    keep_rows = valid_slots.reshape(row_count, 1)
    row_values = full_images.reshape(row_count, model_width).astype(jnp.float32) * keep_rows
    normed1, unit1, inverse1 = norm_rows(row_values, norm1_gain, norm1_shift)
    normed1 = normed1.astype(jnp.bfloat16)
    qkv_bias = jnp.concatenate([qv_bias[0], jnp.zeros_like(qv_bias[0]), qv_bias[1]])
    w_flat = w_qkv.reshape(model_width, 3 * local_width)
    qkv_rows = (jnp.dot(normed1, w_flat, preferred_element_type=jnp.float32) + qkv_bias).astype(
        jnp.bfloat16
    )
    qkv_rows = qkv_rows.reshape(images_here, slot_count, 3, heads_here, HEAD_DIM)
    queries = qkv_rows[:, :, 0]
    key_heads = qkv_rows[:, :, 1]
    value_heads = qkv_rows[:, :, 2]
    key_mask = valid_slots[:, None, None, :] > 0
    scores = scores_of(queries, key_heads, key_mask, score_scale)
    row_top = jnp.max(scores, axis=-1, keepdims=True)
    shifted = jnp.exp(scores - row_top)
    row_total = jnp.sum(shifted, axis=-1, keepdims=True)
    probability = (shifted / row_total).astype(jnp.bfloat16)
    log_total = row_top + jnp.log(row_total)
    mixed = jnp.einsum(
        "bhqk,bkhe->bqhe", probability, value_heads, preferred_element_type=jnp.float32
    ).astype(jnp.bfloat16)
    mixed_rows = mixed.reshape(row_count, local_width)
    attn_part = jnp.dot(mixed_rows, w_proj, preferred_element_type=jnp.float32)
    middle = (
        row_values
        + lax.psum(attn_part.astype(jnp.bfloat16), "tensor").astype(jnp.float32)
        + proj_bias
    )
    normed2, unit2, inverse2 = norm_rows(middle, norm2_gain, norm2_shift)
    normed2 = normed2.astype(jnp.bfloat16)
    pre_act = jnp.dot(normed2, w_fc1, preferred_element_type=jnp.float32) + fc1_bias
    activated = exact_gelu(pre_act).astype(jnp.bfloat16)
    ff_part = jnp.dot(activated, w_fc2, preferred_element_type=jnp.float32)
    ff_share = lax.psum_scatter(
        ff_part.astype(jnp.bfloat16), "tensor", scatter_dimension=1, tiled=True
    ).astype(jnp.float32)
    middle_cols = lax.dynamic_slice_in_dim(middle, first_col, col_count, 1)
    bias_cols = lax.dynamic_slice_in_dim(fc2_bias, first_col, col_count, 0)
    output = ((middle_cols + ff_share + bias_cols) * keep_rows).astype(jnp.bfloat16)
    output = output.reshape(images_here, slot_count, col_count)
    grad_out = full_cot.reshape(row_count, model_width).astype(jnp.float32) * keep_rows
    grad_ff = grad_out.astype(jnp.bfloat16)
    grad_fc2_bias = jnp.sum(grad_ff, axis=0, dtype=jnp.float32)
    grad_w_fc2 = jnp.einsum("rf,rd->fd", activated, grad_ff, preferred_element_type=jnp.float32)
    grad_act = jnp.einsum("rd,fd->rf", grad_ff, w_fc2, preferred_element_type=jnp.float32)
    gelu_pull = jax.vjp(exact_gelu, pre_act)[1]
    grad_pre = gelu_pull(grad_act)[0].astype(jnp.bfloat16)
    grad_fc1_bias = jnp.sum(grad_pre, axis=0, dtype=jnp.float32)
    grad_w_fc1 = jnp.einsum("rd,rf->df", normed2, grad_pre, preferred_element_type=jnp.float32)
    hidden_part = jnp.einsum("rf,df->rd", grad_pre, w_fc1, preferred_element_type=jnp.float32)
    grad_normed2 = lax.psum(hidden_part.astype(jnp.bfloat16), "tensor").astype(jnp.float32)
    grad_norm2_gain = jnp.sum(grad_normed2 * unit2, axis=0)
    grad_norm2_shift = jnp.sum(grad_normed2, axis=0)
    grad_middle = grad_out + norm_back(grad_normed2, unit2, inverse2, norm2_gain)
    grad_attn = grad_middle.astype(jnp.bfloat16)
    grad_proj_bias = jnp.sum(grad_attn, axis=0, dtype=jnp.float32)
    grad_w_proj = jnp.einsum("rc,rd->cd", mixed_rows, grad_attn, preferred_element_type=jnp.float32)
    grad_mixed = jnp.einsum(
        "rd,cd->rc", grad_attn, w_proj, preferred_element_type=jnp.float32
    ).astype(jnp.bfloat16)
    grad_mixed = grad_mixed.reshape(images_here, slot_count, heads_here, HEAD_DIM)
    scores_again = scores_of(queries, key_heads, key_mask, score_scale)
    weights_soft = jnp.exp(scores_again - log_total)
    grad_value = jnp.einsum(
        "bhqk,bqhe->bkhe",
        weights_soft.astype(jnp.bfloat16),
        grad_mixed,
        preferred_element_type=jnp.float32,
    )
    grad_prob = jnp.einsum(
        "bqhe,bkhe->bhqk", grad_mixed, value_heads, preferred_element_type=jnp.float32
    )
    row_dot = jnp.sum(weights_soft * grad_prob, axis=-1, keepdims=True)
    grad_scores = (weights_soft * (grad_prob - row_dot)).astype(jnp.bfloat16)
    grad_query = (
        jnp.einsum("bhqk,bkhe->bqhe", grad_scores, key_heads, preferred_element_type=jnp.float32)
        * score_scale
    )
    grad_key = (
        jnp.einsum("bhqk,bqhe->bkhe", grad_scores, queries, preferred_element_type=jnp.float32)
        * score_scale
    )
    grad_qkv = jnp.stack([grad_query, grad_key, grad_value], axis=2).astype(jnp.bfloat16)
    grad_qkv = grad_qkv.reshape(row_count, 3 * local_width)
    bias_sums = jnp.sum(grad_qkv, axis=0, dtype=jnp.float32).reshape(3, local_width)
    grad_qv_bias = jnp.stack([bias_sums[0], bias_sums[2]])
    grad_w_qkv = jnp.einsum("rd,rc->dc", normed1, grad_qkv, preferred_element_type=jnp.float32)
    grad_w_qkv = grad_w_qkv.reshape(model_width, 3, local_width)
    normed_part = jnp.einsum("rc,dc->rd", grad_qkv, w_flat, preferred_element_type=jnp.float32)
    grad_normed1 = lax.psum(normed_part.astype(jnp.bfloat16), "tensor").astype(jnp.float32)
    grad_norm1_gain = jnp.sum(grad_normed1 * unit1, axis=0)
    grad_norm1_shift = jnp.sum(grad_normed1, axis=0)
    grad_full = grad_middle + norm_back(grad_normed1, unit1, inverse1, norm1_gain)
    grad_input = lax.dynamic_slice_in_dim(grad_full, first_col, col_count, 1) * keep_rows
    input_grad = grad_input.astype(jnp.bfloat16).reshape(images_here, slot_count, col_count)
    summed = (
        lax.psum(grad_norm1_gain.astype(jnp.bfloat16), "dp").astype(jnp.float32),
        lax.psum(grad_norm1_shift.astype(jnp.bfloat16), "dp").astype(jnp.float32),
        lax.psum(grad_w_qkv.astype(jnp.bfloat16), "dp").astype(jnp.float32),
        lax.psum(grad_qv_bias.astype(jnp.bfloat16), "dp").astype(jnp.float32),
        lax.psum(grad_w_proj.astype(jnp.bfloat16), "dp").astype(jnp.float32),
        lax.psum(grad_proj_bias.astype(jnp.bfloat16), "dp").astype(jnp.float32),
        lax.psum(grad_norm2_gain.astype(jnp.bfloat16), "dp").astype(jnp.float32),
        lax.psum(grad_norm2_shift.astype(jnp.bfloat16), "dp").astype(jnp.float32),
        lax.psum(grad_w_fc1.astype(jnp.bfloat16), "dp").astype(jnp.float32),
        lax.psum(grad_fc1_bias.astype(jnp.bfloat16), "dp").astype(jnp.float32),
        lax.psum(grad_w_fc2.astype(jnp.bfloat16), "dp").astype(jnp.float32),
        lax.psum(grad_fc2_bias.astype(jnp.bfloat16), "dp").astype(jnp.float32),
    )
    return (
        output,
        input_grad,
        summed[0],
        summed[1],
        summed[2],
        summed[3],
        summed[4],
        summed[5],
        summed[6],
        summed[7],
        summed[8],
        summed[9],
        summed[10],
        summed[11],
    )


def solution(mesh):
    in_specs = (
        P("dp", None, "tensor"),
        P("dp"),
        P("dp", None, "tensor"),
        P(),
        P(),
        P(None, None, "tensor"),
        P(None, "tensor"),
        P("tensor", None),
        P(),
        P(),
        P(),
        P(None, "tensor"),
        P("tensor"),
        P("tensor", None),
        P(),
    )
    out_specs = (
        P("dp", None, "tensor"),
        P("dp", None, "tensor"),
        P(),
        P(),
        P(None, None, "tensor"),
        P(None, "tensor"),
        P("tensor", None),
        P(),
        P(),
        P(),
        P(None, "tensor"),
        P("tensor"),
        P("tensor", None),
        P(),
    )
    return jax.shard_map(
        per_device, mesh=mesh, in_specs=in_specs, out_specs=out_specs, check_vma=False
    )
```

profile of v0, /device:TPU:0, one launch (start us, length us, event | category | flops | bytes accessed | tf_op | source)
XLA Modules:
  0.0 699.4 jit_solution(9213317824829638723)
XLA Ops:
  10.2 2.6 copy.39
  12.8 54.3 %all-gather.3.cloned.1.call-done = bf16[4,320,1024]{2,1,0:T(8,128)(2,1)} async-done(((bf16[4,320,256]{2,1,0:T(8,128)(2,1)}), bf16[4,320,1024]{2,1,0:T(8,128)(2,1)}) %all-gather.3.cloned.1.call-update) | async-done | bytes 2621456 | tf_op jit(solution)/shard_map/all_gather | solution.py:64
  67.2 2.6 fusion.18
  69.8 2.8 multiply_reduce_fusion.3
  75.4 3.5 add_convert_fusion.3
  78.9 6.7 reshape.265
  85.6 4.0 fusion.57
  89.6 2.3 copy.64
  91.8 2.5 copy.65
  94.3 3.2 copy.66
  97.5 3.2 fusion.24
  102.7 2.4 fusion.35
  108.7 3.4 convolution_convert_fusion.1
  112.3 9.5 %all-gather.5.cloned.1.call-done = bf16[4,320,1024]{2,1,0:T(8,128)(2,1)} async-done(((bf16[4,320,256]{2,1,0:T(8,128)(2,1)}), bf16[4,320,1024]{2,1,0:T(8,128)(2,1)}) %all-gather.5.cloned.1.call-update) | async-done | bytes 2621456 | tf_op jit(solution)/shard_map/all_gather | solution.py:65
  121.8 105.2 %all-reduce.7.cloned.1.call-done = bf16[1280,1024]{1,0:T(8,128)(2,1)} async-done(((bf16[1280,1024]{1,0:T(8,128)(2,1)}), bf16[1280,1024]{1,0:T(8,128)(2,1)}) %all-reduce.7.cloned.1.call-update) | async-done | bytes 2621456 | tf_op jit(solution)/shard_map/psum | solution.py:96
  227.0 5.0 fusion.56
  232.8 2.5 copy-done.48
  235.3 3.0 fusion.51
  238.4 16.8 %fusion.52 = (bf16[1024]{0:T(1024)(128)(2,1)}, bf16[1280,1024]{1,0:T(8,128)(2,1)S(1)}, f32[1280,1024]{1,0:T(8,128)}) fusion(f32[1280,1024]{1,0:T(8,128)S(1)} %fusion.51, f32[1024]{0:T(1024)S(1)} %copy-done.45, bf16[1280,1024]{1,0:T(8,128)(2,1)S(1)} %get-tuple-element.49, bf16[1024,1024]{1,0:T(8,128)(2,1)S(1)} %copy-done), kind=kOutput, calls=%fused_computation.113 | convolution fusion | flops 2781346816 | bytes 17831936 | tf_op jit(solution)/shard_map/rd,fd->rf/dot_general | solution.py:115
  256.6 4.2 convolution_convert_fusion.2
  262.3 101.8 %all-reduce.9.cloned.1.call-done = bf16[1280,1024]{1,0:T(8,128)(2,1)} async-done(((bf16[1280,1024]{1,0:T(8,128)(2,1)}), bf16[1280,1024]{1,0:T(8,128)(2,1)}) %all-reduce.9.cloned.1.call-update) | async-done | bytes 2621456 | tf_op jit(solution)/shard_map/psum | solution.py:121
  364.1 5.5 fusion.9
  369.6 5.6 convert_reduce_fusion
  375.2 2.3 copy-done.4
  379.2 3.1 reshape.266
  382.3 3.2 copy.47
  385.5 5.5 fusion.27
  391.1 5.4 multiply_reduce_fusion
  396.5 2.9 multiply_convert_fusion
  402.2 3.2 copy.52
  405.5 4.7 convert_element_type.226
  410.2 5.7 convolution_convert_fusion
  416.0 5.5 multiply_convert_fusion.2
  423.0 4.1 convolution_convert_fusion.3
  427.4 7.1 %convolution_convert_fusion.5 = bf16[1024,1024]{1,0:T(8,128)(2,1)} fusion(bf16[1280,1024]{1,0:T(8,128)(2,1)} %copy-done.15, bf16[1280,1024]{1,0:T(8,128)(2,1)} %copy-done.12), kind=kOutput, calls=%fused_computation.66 | convolution fusion | flops 2685403136 | bytes 7340032 | tf_op jit(solution)/shard_map/rf,rd->fd/dot_general | solution.py:114
  434.5 7.3 %convolution_convert_fusion.6 = bf16[1024,1024]{1,0:T(8,128)(2,1)} fusion(bf16[1280,1024]{1,0:T(8,128)(2,1)S(1)} %copy-done.52, f32[1280,1024]{1,0:T(8,128)} %copy-done.2, f32[1024]{0:T(1024)S(1)} %copy-done.50, f32[1024]{0:T(1024)S(1)} %copy-done.38, f32[1280]{0:T(1024)S(1)} %copy-done.31, f32[1280]{0:T(1024)S(1)} %copy-done.25), kind=kOutput, calls=%fused_computation.67 | convolution fusion | flops 2691956736 | bytes 9979904 | tf_op jit(solution)/shard_map/rd,rf->df/dot_general | solution.py:119
  444.4 3.4 convolution_convert_fusion.7
  448.8 2.3 fusion.25
  451.3 67.9 %all-reduce.11.cloned.1.call-done = bf16[1280,1024]{1,0:T(8,128)(2,1)} async-done(((bf16[1280,1024]{1,0:T(8,128)(2,1)}), bf16[1280,1024]{1,0:T(8,128)(2,1)}) %all-reduce.11.cloned.1.call-update) | async-done | bytes 2621456 | tf_op jit(solution)/shard_map/psum | solution.py:160
  521.4 7.4 %fusion.10 = (bf16[1024]{0:T(1024)(128)(2,1)S(1)}, f32[1280]{0:T(1024)S(1)}, f32[1280]{0:T(1024)S(1)}, f32[1280,1024]{1,0:T(8,128)}, f32[1280,1024]{1,0:T(8,128)}) fusion(bf16[1280,1024]{1,0:T(8,128)(2,1)} %all-reduce.11.cloned.1.call-done, f32[1280]{0:T(1024)S(1)} %rsqrt.22, f32[1280]{0:T(1024)S(1)} %div.43, f32[1280]{0:T(1024)S(1)} %reshape.262, ...), kind=kLoop, calls=%fused_computation.21 | loop fusion | flops 14414336 | bytes 15760384 | tf_op jit(solution)/shard_map/reduce_sum | solution.py:161
  528.9 24.7 %all-reduce = (bf16[1024]{0:T(1024)(128)(2,1)S(1)}, bf16[1024]{0:T(1024)(128)(2,1)S(1)}, bf16[2,256]{1,0:T(2,128)(2,1)S(1)}, bf16[1024]{0:T(1024)(128)(2,1)S(1)}...) all-reduce(bf16[1024]{0:T(1024)(128)(2,1)S(1)} %get-tuple-element.1, ...), channel_id=1, replica_groups=mesh['dp'=8,'tensor'=4] {'dp'}, use_global_device_ids=true, to_apply=%region_16.17 | all-reduce | flops 7680 | bytes 30720 | tf_op jit(solution)/shard_map/psum | solution.py:167
  558.3 14.9 %reduce-scatter.2.cloned.1.call-done = bf16[1280,256]{1,0:T(8,128)(2,1)} async-done(((bf16[1280,1024]{1,0:T(8,128)(2,1)}), bf16[1280,256]{1,0:T(8,128)(2,1)}) %reduce-scatter.2.cloned.1.call-update) | async-done | bytes 655376 | tf_op jit(solution)/shard_map/reduce_scatter | solution.py:104
  573.2 4.1 fusion.32
  577.3 104.3 %all-reduce.13.cloned.1.call-done = (bf16[1024,3,256]{2,0,1:T(8,128)(2,1)}, bf16[256,1024]{1,0:T(8,128)(2,1)}, bf16[1024,1024]{1,0:T(8,128)(2,1)}, bf16[1024,1024]{1,0:T(8,128)(2,1)}) async-done(((bf16[1024,3,256]{2,0,1:T(8,128)(2,1)}, bf16[256,1024]{1,0:T(8,128)(2,1)}, bf16[1024,1024]{1,0:T(8,128)(2,1)}, bf16[1024,1024]{1,0:T(8,128)(2,1)}), (bf16[1024,3,256]{2,0,1:T(8,128)(2,1)}, ...) | async-done | bytes 6291472 | tf_op jit(solution)/shard_map/psum | solution.py:169
  681.6 2.3 convert_element_type.238
  683.9 3.5 convert_element_type.234
  687.4 2.5 convert_element_type.244
  689.8 2.5 convert_element_type.247
  (167 shorter events, 32.1 us)
Async XLA Ops:
  7.2 231.2 %copy-start = (bf16[1024,1024]{1,0:T(8,128)(2,1)S(1)}, bf16[1024,1024]{1,0:T(8,128)(2,1)}, u32[]{:S(2)}) copy-start(bf16[1024,1024]{1,0:T(8,128)(2,1)} %param.28) | copy-start | bytes 6291460
  7.2 65.4 %copy-start.39 = (f32[1024]{0:T(1024)S(1)}, f32[1024]{0:T(1024)}, u32[]{:S(2)}) copy-start(f32[1024]{0:T(1024)} %param.18) | copy-start | bytes 12292
  7.2 65.3 %copy-start.44 = (f32[1024]{0:T(1024)S(1)}, f32[1024]{0:T(1024)}, u32[]{:S(2)}) copy-start(f32[1024]{0:T(1024)} %param.19) | copy-start | bytes 12292
  7.2 60.0 %all-gather.3.cloned.1.call-start = ((), (), s32[]{:S(2)}) async-start(), calls=%async_computation.1 | async-start | bytes 3276800 | tf_op jit(solution)/shard_map/all_gather | solution.py:64
  8.0 113.8 %all-gather.5.cloned.1.call-start = ((), (), s32[]{:S(2)}) async-start(), calls=%async_computation.4 | async-start | bytes 3276800 | tf_op jit(solution)/shard_map/all_gather | solution.py:65
  8.7 218.3 %all-reduce.7.cloned.1.call-start = ((), (), s32[]{:S(2)}) async-start(), calls=%async_computation.2 | async-start | bytes 5242880 | tf_op jit(solution)/shard_map/psum | solution.py:96
  10.2 92.5 %copy-start.34 = (pred[4,320]{1,0:T(4,128)(4,1)}, pred[4,320]{1,0:T(4,128)(4,1)S(1)}, u32[]{:S(2)}) copy-start(pred[4,320]{1,0:T(4,128)(4,1)S(1)} %get-tuple-element.54) | copy-start | bytes 3844
  67.2 5.4 copy-start.3
  67.2 8.2 %copy-start.20 = (bf16[1024,3,256]{0,2,1:T(8,128)(2,1)S(1)}, bf16[1024,3,256]{0,2,1:T(8,128)(2,1)}, u32[]{:S(2)}) copy-start(bf16[1024,3,256]{0,2,1:T(8,128)(2,1)} %copy.39) | copy-start | bytes 4718596
  69.7 4.1 copy-start.26
  100.7 4.4 copy-start.1
  100.8 4.4 copy-start.22
  112.2 251.9 %all-reduce.9.cloned.1.call-start = ((), (), s32[]{:S(2)}) async-start(), calls=%async_computation.5 | async-start | bytes 5242880 | tf_op jit(solution)/shard_map/psum | solution.py:121
  232.0 6.3 copy-start.2
  232.0 6.3 copy-start.12
  232.0 3.2 copy-start.48
  232.1 6.2 copy-start.23
  238.3 16.8 %copy-start.8 = (f32[1280,1024]{1,0:T(8,128)}, f32[1280,1024]{1,0:T(8,128)S(1)}, u32[]{:S(2)}) copy-start(f32[1280,1024]{1,0:T(8,128)S(1)} %fusion.51) | copy-start | bytes 15728644
  260.9 258.3 %all-reduce.11.cloned.1.call-start = ((), (), s32[]{:S(2)}) async-start(), calls=%async_computation.6 | async-start | bytes 5242880 | tf_op jit(solution)/shard_map/psum | solution.py:160
  364.1 5.5 copy-start.5
  364.1 5.5 copy-start.6
  364.1 5.5 copy-start.24
  364.1 5.5 copy-start.30
  364.1 5.5 copy-start.37
  369.6 7.8 %copy-start.18 = (bf16[256,1024]{1,0:T(8,128)(2,1)S(1)}, bf16[256,1024]{1,0:T(8,128)(2,1)}, u32[]{:S(2)}) copy-start(bf16[256,1024]{1,0:T(8,128)(2,1)} %param.22) | copy-start | bytes 1572868
  385.5 5.5 copy-start.10
  385.5 5.6 copy-start.11
  385.5 5.6 copy-start.21
  385.5 5.6 copy-start.35
  385.5 11.0 %slice-start = ((s8[7864320]{0:T(1024)(128)(4,1)}), s8[4194304]{0:T(1024)(128)(4,1)S(1)}, s32[]{:S(2)}) async-start(s8[7864320]{0:T(1024)(128)(4,1)} %bitcast.95), calls=%async_computation.8 | async-start | bytes 8388608
  391.1 5.4 slice-start.1
  410.2 5.8 copy-start.46
  415.9 157.3 %reduce-scatter.2.cloned.1.call-start = ((), (), s32[]{:S(2)}) async-start(), calls=%async_computation.3 | async-start | bytes 3276800 | tf_op jit(solution)/shard_map/reduce_scatter | solution.py:104
  427.1 7.3 %copy-start.25 = (f32[1280]{0:T(1024)S(1)}, f32[1280]{0:T(1024)}, u32[]{:S(2)}) copy-start(f32[1280]{0:T(1024)} %copy-done.23) | copy-start | bytes 15364
  427.1 7.3 %copy-start.31 = (f32[1280]{0:T(1024)S(1)}, f32[1280]{0:T(1024)}, u32[]{:S(2)}) copy-start(f32[1280]{0:T(1024)} %copy-done.29) | copy-start | bytes 15364
  427.1 7.3 %copy-start.38 = (f32[1024]{0:T(1024)S(1)}, f32[1024]{0:T(1024)}, u32[]{:S(2)}) copy-start(f32[1024]{0:T(1024)} %param.24) | copy-start | bytes 12292
  427.2 7.3 %copy-start.50 = (f32[1024]{0:T(1024)S(1)}, f32[1024]{0:T(1024)}, u32[]{:S(2)}) copy-start(f32[1024]{0:T(1024)} %param.25) | copy-start | bytes 12292
  427.2 254.4 %all-reduce.13.cloned.1.call-start = ((), (), s32[]{:S(2)}) async-start(), calls=%async_computation.7 | async-start | bytes 12582912 | tf_op jit(solution)/shard_map/psum | solution.py:169
  427.4 7.1 %copy-start.52 = (bf16[1280,1024]{1,0:T(8,128)(2,1)S(1)}, bf16[1280,1024]{1,0:T(8,128)(2,1)}, u32[]{:S(2)}) copy-start(bf16[1280,1024]{1,0:T(8,128)(2,1)} %copy-done.51) | copy-start | bytes 7864324
  427.4 14.4 %slice-start.2 = ((s8[5242880]{0:T(1024)(128)(4,1)}), s8[4194304]{0:T(1024)(128)(4,1)S(1)}, s32[]{:S(2)}) async-start(s8[5242880]{0:T(1024)(128)(4,1)} %bitcast.97), calls=%async_computation.10 | async-start | bytes 8388608
  434.5 7.3 %slice-start.3 = ((s8[5242880]{0:T(1024)(128)(4,1)}), s8[1048576]{0:T(1024)(128)(4,1)S(1)}, s32[]{:S(2)}) async-start(s8[5242880]{0:T(1024)(128)(4,1)} %bitcast.97), calls=%async_computation.11 | async-start | bytes 2097152
  447.8 73.6 %copy-start.40 = (f32[1024]{0:T(1024)S(1)}, f32[1024]{0:T(1024)}, u32[]{:S(2)}) copy-start(f32[1024]{0:T(1024)} %param.18) | copy-start | bytes 12292
  521.4 7.5 %copy-start.41 = (bf16[1024]{0:T(1024)(128)(2,1)S(1)}, bf16[1024]{0:T(1024)(128)(2,1)}, u32[]{:S(2)}) copy-start(bf16[1024]{0:T(1024)(128)(2,1)} %get-tuple-element.35) | copy-start | bytes 6148
  521.4 7.5 %copy-start.42 = (bf16[1024]{0:T(1024)(128)(2,1)S(1)}, bf16[1024]{0:T(1024)(128)(2,1)}, u32[]{:S(2)}) copy-start(bf16[1024]{0:T(1024)(128)(2,1)} %get-tuple-element.46) | copy-start | bytes 6148
  521.4 7.5 %copy-start.43 = (bf16[1024]{0:T(1024)(128)(2,1)S(1)}, bf16[1024]{0:T(1024)(128)(2,1)}, u32[]{:S(2)}) copy-start(bf16[1024]{0:T(1024)(128)(2,1)} %get-tuple-element.14) | copy-start | bytes 6148
  521.4 7.5 %copy-start.47 = (bf16[1024]{0:T(1024)(128)(2,1)S(1)}, bf16[1024]{0:T(1024)(128)(2,1)}, u32[]{:S(2)}) copy-start(bf16[1024]{0:T(1024)(128)(2,1)} %get-tuple-element.32) | copy-start | bytes 6148
  681.6 5.8 copy-start.17
  683.9 6.0 copy-start.16
  (16 other events, 30.0 us)
Sparse Core Ops, SparseCore 0:
  9.6 57.5 all-gather.2
  68.7 52.9 all-gather.4
  124.7 102.2 all-reduce.6
  261.0 103.0 all-reduce.8
  416.1 103.0 all-reduce.10
  521.9 51.2 reduce-scatter.1
  578.0 103.5 all-reduce.12
where the time goes:
time: 709 us; the launch traced here: 699 us
  waiting for transfers between devices  459 us (65%)
  matrix products  80.7 us (11%)
  other arithmetic  67.8 us (10%)
  local copies, waits for them, and re-layouts  51.3 us (7%)
  blocking collectives  24.7 us (3%)
  between operations  15.1 us (2%)
    psum x1, waiting for transfers between devices, per_device(): lax.psum(attn_part.astype(jnp.bfloat16), 'tensor').astype(jnp.float32)  105 us
    psum x1, waiting for transfers between devices, per_device(): lax.psum(grad_w_qkv.astype(jnp.bfloat16), 'dp').astype(jnp.float32)  104 us
    psum x1, waiting for transfers between devices, per_device(): lax.psum(hidden_part.astype(jnp.bfloat16), 'tensor').astype(jnp.float32)  102 us
    psum x1, waiting for transfers between devices, per_device(): lax.psum(normed_part.astype(jnp.bfloat16), 'tensor').astype(jnp.float32)  67.9 us
    all_gather x1, waiting for transfers between devices, per_device(): lax.all_gather(images, 'tensor', axis=2, tiled=True)  54.3 us
    psum x1, blocking collectives, per_device(): lax.psum(grad_norm1_gain.astype(jnp.bfloat16), 'dp').astype(jnp.float32)  24.7 us
    unnamed x118, local copies, waits for them, and re-layouts  20.9 us
    dot_general x1, matrix products, per_device(): jnp.einsum('rd,fd->rf', grad_ff, w_fc2, preferred_element_type=jnp.float32)  16.8 us
  transfers between devices with their start and end apart: 7, of which 7 were waited for; matrix products, arithmetic and copies ran while one was open for 14% of the time, Pallas kernels for 0%

commit v1 on v0

--- a/solution.py
+++ b/solution.py
@@ -93,7 +93,9 @@
     attn_part = jnp.dot(mixed_rows, w_proj, preferred_element_type=jnp.float32)
     middle = (
         row_values
-        + lax.psum(attn_part.astype(jnp.bfloat16), "tensor").astype(jnp.float32)
+        + jnp.sum(lax.all_gather(attn_part.astype(jnp.bfloat16), "tensor"), axis=0).astype(
+            jnp.float32
+        )
         + proj_bias
     )
     normed2, unit2, inverse2 = norm_rows(middle, norm2_gain, norm2_shift)

time: 709 us -> 827 us (1.17)
  waiting for transfers between devices: 459 us -> 558 us
  other arithmetic: 67.8 us -> 87.2 us
    all_gather x0 -> x1, waiting for transfers between devices: none -> 181 us  [per_device(): lax.all_gather(attn_part.astype(jnp.bfloat16), 'tensor')]
    psum x1 -> x0, waiting for transfers between devices: 105 us -> none  [per_device(): lax.psum(attn_part.astype(jnp.bfloat16), 'tensor').astype(jnp.float32)]
    all_gather x1, waiting for transfers between devices: 9.45 us -> 31.4 us  [per_device(): lax.all_gather(cotangent, 'tensor', axis=2, tiled=True)]
    reduce_sum x0 -> x1, other arithmetic: none -> 8.97 us  [per_device(): jnp.sum(lax.all_gather(attn_part.astype(jnp.bfloat16), 'tensor'), axis=0)]
  transfers between devices with their start and end apart: 7 -> 7, of which waited for: 7 -> 7; matrix products, arithmetic and copies ran while one was open for 14% -> 10% of each run, Pallas kernels for 0% -> 0%
where the time goes in v1:
time: 827 us; the launch traced here: 817 us
  waiting for transfers between devices  558 us (67%)
  other arithmetic  87.2 us (11%)
  matrix products  80.7 us (10%)
  local copies, waits for them, and re-layouts  51.7 us (6%)
  blocking collectives  24.7 us (3%)
  between operations  15.1 us (2%)
    all_gather x1, waiting for transfers between devices, per_device(): lax.all_gather(attn_part.astype(jnp.bfloat16), 'tensor')  181 us
    psum x1, waiting for transfers between devices, per_device(): lax.psum(grad_w_qkv.astype(jnp.bfloat16), 'dp').astype(jnp.float32)  104 us
    psum x1, waiting for transfers between devices, per_device(): lax.psum(hidden_part.astype(jnp.bfloat16), 'tensor').astype(jnp.float32)  101 us
    psum x1, waiting for transfers between devices, per_device(): lax.psum(normed_part.astype(jnp.bfloat16), 'tensor').astype(jnp.float32)  68 us
    all_gather x1, waiting for transfers between devices, per_device(): lax.all_gather(images, 'tensor', axis=2, tiled=True)  55.1 us
    all_gather x1, waiting for transfers between devices, per_device(): lax.all_gather(cotangent, 'tensor', axis=2, tiled=True)  31.4 us
    psum x1, blocking collectives, per_device(): lax.psum(grad_norm1_gain.astype(jnp.bfloat16), 'dp').astype(jnp.float32)  24.7 us
    unnamed x118, local copies, waits for them, and re-layouts  18.5 us
  transfers between devices with their start and end apart: 7, of which 7 were waited for; matrix products, arithmetic and copies ran while one was open for 10% of the time, Pallas kernels for 0%

profile of v1, /device:TPU:0, one launch (start us, length us, event | category | flops | bytes accessed | tf_op | source)
XLA Modules:
  0.0 817.4 jit_solution(1606800124437384962)
XLA Ops:
  8.0 2.6 copy.39
  12.1 55.1 %all-gather.5.cloned.1.call-done = bf16[4,320,1024]{2,1,0:T(8,128)(2,1)} async-done(((bf16[4,320,256]{2,1,0:T(8,128)(2,1)}), bf16[4,320,1024]{2,1,0:T(8,128)(2,1)}) %all-gather.5.cloned.1.call-update) | async-done | bytes 2621456 | tf_op jit(solution)/shard_map/all_gather | solution.py:64
  67.2 2.6 fusion.18
  69.8 2.8 multiply_reduce_fusion.3
  75.4 3.5 add_convert_fusion.3
  78.9 6.7 reshape.309
  85.6 3.9 fusion.57
  91.8 2.5 copy.65
  94.3 3.2 copy.66
  97.5 3.2 fusion.24
  102.7 2.4 fusion.36
  108.7 3.4 convolution_convert_fusion.1
  113.0 181.4 %all-gather.9.cloned.1.call-done = bf16[5120,1024]{1,0:T(8,128)(2,1)} async-done(((bf16[1280,1024]{1,0:T(8,128)(2,1)}), bf16[5120,1024]{1,0:T(8,128)(2,1)}) %all-gather.9.cloned.1.call-update) | async-done | bytes 10485776 | tf_op jit(solution)/shard_map/all_gather | solution.py:96
  294.3 9.0 %reduce_sum.192 = bf16[1280,1024]{1,0:T(8,128)(2,1)} reduce(bf16[4,1280,1024]{2,1,0:T(8,128)(2,1)} %bitcast.102, bf16[]{:T(256)} %constant.17.clone.1), dimensions={0}, to_apply=%region_4.5 | reduce | flops 3932160 | bytes 13107202 | tf_op jit(solution)/shard_map/reduce_sum | solution.py:96
  303.3 6.2 fusion.25
  311.5 4.1 multiply_reduce_fusion.2
  317.6 31.4 %all-gather.7.cloned.1.call-done = bf16[4,320,1024]{2,1,0:T(8,128)(2,1)} async-done(((bf16[4,320,256]{2,1,0:T(8,128)(2,1)}), bf16[4,320,1024]{2,1,0:T(8,128)(2,1)}) %all-gather.7.cloned.1.call-update) | async-done | bytes 2621456 | tf_op jit(solution)/shard_map/all_gather | solution.py:65
  349.0 4.8 add_add_fusion.1
  353.9 3.1 fusion.52
  357.0 16.8 %fusion.53 = (bf16[1024]{0:T(1024)(128)(2,1)}, bf16[1280,1024]{1,0:T(8,128)(2,1)S(1)}, f32[1280,1024]{1,0:T(8,128)}) fusion(f32[1280,1024]{1,0:T(8,128)S(1)} %fusion.52, f32[1024]{0:T(1024)S(1)} %copy-done.45, bf16[1280,1024]{1,0:T(8,128)(2,1)S(1)} %get-tuple-element.50, bf16[1024,1024]{1,0:T(8,128)(2,1)S(1)} %copy-done), kind=kOutput, calls=%fused_computation.115 | convolution fusion | flops 2781346816 | bytes 17831936 | tf_op jit(solution)/shard_map/rd,fd->rf/dot_general | solution.py:117
  375.4 4.2 convolution_convert_fusion.2
  381.1 101.0 %all-reduce.6.cloned.1.call-done = bf16[1280,1024]{1,0:T(8,128)(2,1)} async-done(((bf16[1280,1024]{1,0:T(8,128)(2,1)}), bf16[1280,1024]{1,0:T(8,128)(2,1)}) %all-reduce.6.cloned.1.call-update) | async-done | bytes 2621456 | tf_op jit(solution)/shard_map/psum | solution.py:123
  482.1 5.5 fusion.9
  487.6 5.6 convert_reduce_fusion
  493.2 2.3 copy-done.4
  497.2 3.1 reshape.310
  500.3 3.2 copy.47
  503.6 5.5 fusion.28
  509.2 5.4 multiply_reduce_fusion
  514.6 2.9 multiply_convert_fusion
  520.3 3.2 copy.52
  523.5 4.7 convert_element_type.239
  528.3 5.7 convolution_convert_fusion
  534.1 5.5 multiply_convert_fusion.2
  541.0 4.1 convolution_convert_fusion.3
  545.4 7.0 convolution_convert_fusion.5
  552.5 7.3 convolution_convert_fusion.6
  562.4 3.4 convolution_convert_fusion.7
  566.8 2.3 fusion.26
  569.3 68.0 %all-reduce.8.cloned.1.call-done = bf16[1280,1024]{1,0:T(8,128)(2,1)} async-done(((bf16[1280,1024]{1,0:T(8,128)(2,1)}), bf16[1280,1024]{1,0:T(8,128)(2,1)}) %all-reduce.8.cloned.1.call-update) | async-done | bytes 2621456 | tf_op jit(solution)/shard_map/psum | solution.py:162
  639.5 7.2 fusion.10
  646.7 24.7 %all-reduce = (bf16[1024]{0:T(1024)(128)(2,1)S(1)}, bf16[1024]{0:T(1024)(128)(2,1)S(1)}, bf16[2,256]{1,0:T(2,128)(2,1)S(1)}, bf16[1024]{0:T(1024)(128)(2,1)S(1)}...) all-reduce(bf16[1024]{0:T(1024)(128)(2,1)S(1)} %get-tuple-element.1, ...), channel_id=1, replica_groups=mesh['dp'=8,'tensor'=4] {'dp'}, use_global_device_ids=true, to_apply=%region_16.17 | all-reduce | flops 7680 | bytes 30720 | tf_op jit(solution)/shard_map/psum | solution.py:169
  676.2 15.1 %reduce-scatter.2.cloned.1.call-done = bf16[1280,256]{1,0:T(8,128)(2,1)} async-done(((bf16[1280,1024]{1,0:T(8,128)(2,1)}), bf16[1280,256]{1,0:T(8,128)(2,1)}) %reduce-scatter.2.cloned.1.call-update) | async-done | bytes 655376 | tf_op jit(solution)/shard_map/reduce_scatter | solution.py:106
  691.3 4.1 fusion.33
  695.4 104.3 %all-reduce.10.cloned.1.call-done = (bf16[1024,3,256]{2,0,1:T(8,128)(2,1)}, bf16[256,1024]{1,0:T(8,128)(2,1)}, bf16[1024,1024]{1,0:T(8,128)(2,1)}, bf16[1024,1024]{1,0:T(8,128)(2,1)}) async-done(((bf16[1024,3,256]{2,0,1:T(8,128)(2,1)}, bf16[256,1024]{1,0:T(8,128)(2,1)}, bf16[1024,1024]{1,0:T(8,128)(2,1)}, bf16[1024,1024]{1,0:T(8,128)(2,1)}), (bf16[1024,3,256]{2,0,1:T(8,128)(2,1)}, ...) | async-done | bytes 6291472 | tf_op jit(solution)/shard_map/psum | solution.py:171
  801.9 3.5 convert_element_type.247
  805.4 2.5 convert_element_type.257
  807.9 2.5 convert_element_type.260
  (171 shorter events, 40.0 us)
Async XLA Ops:
  7.2 349.8 %copy-start = (bf16[1024,1024]{1,0:T(8,128)(2,1)S(1)}, bf16[1024,1024]{1,0:T(8,128)(2,1)}, u32[]{:S(2)}) copy-start(bf16[1024,1024]{1,0:T(8,128)(2,1)} %param.28) | copy-start | bytes 6291460
  7.2 65.3 %copy-start.39 = (f32[1024]{0:T(1024)S(1)}, f32[1024]{0:T(1024)}, u32[]{:S(2)}) copy-start(f32[1024]{0:T(1024)} %param.18) | copy-start | bytes 12292
  7.2 65.3 %copy-start.44 = (f32[1024]{0:T(1024)S(1)}, f32[1024]{0:T(1024)}, u32[]{:S(2)}) copy-start(f32[1024]{0:T(1024)} %param.19) | copy-start | bytes 12292
  7.2 60.0 %all-gather.5.cloned.1.call-start = ((), (), s32[]{:S(2)}) async-start(), calls=%async_computation.1 | async-start | bytes 3276800 | tf_op jit(solution)/shard_map/all_gather | solution.py:64
  8.0 286.4 %all-gather.9.cloned.1.call-start = ((), (), s32[]{:S(2)}) async-start(), calls=%async_computation.6 | async-start | bytes 13107200 | tf_op jit(solution)/shard_map/all_gather | solution.py:96
  12.1 90.6 %copy-start.34 = (pred[4,320]{1,0:T(4,128)(4,1)}, pred[4,320]{1,0:T(4,128)(4,1)S(1)}, u32[]{:S(2)}) copy-start(pred[4,320]{1,0:T(4,128)(4,1)S(1)} %get-tuple-element.55) | copy-start | bytes 3844
  67.2 5.4 copy-start.1
  67.2 8.2 %copy-start.20 = (bf16[1024,3,256]{0,2,1:T(8,128)(2,1)S(1)}, bf16[1024,3,256]{0,2,1:T(8,128)(2,1)}, u32[]{:S(2)}) copy-start(bf16[1024,3,256]{0,2,1:T(8,128)(2,1)} %copy.39) | copy-start | bytes 4718596
  100.7 4.4 copy-start.2
  100.7 4.4 copy-start.22
  112.1 236.8 %all-gather.7.cloned.1.call-start = ((), (), s32[]{:S(2)}) async-start(), calls=%async_computation.3 | async-start | bytes 3276800 | tf_op jit(solution)/shard_map/all_gather | solution.py:65
  112.9 369.2 %all-reduce.6.cloned.1.call-start = ((), (), s32[]{:S(2)}) async-start(), calls=%async_computation.4 | async-start | bytes 5242880 | tf_op jit(solution)/shard_map/psum | solution.py:123
  349.0 4.9 copy-start.26
  349.0 4.9 copy-start.29
  349.0 4.9 copy-start.36
  349.0 4.9 copy-start.48
  349.0 4.9 copy-start.49
  357.0 16.9 %copy-start.8 = (f32[1280,1024]{1,0:T(8,128)}, f32[1280,1024]{1,0:T(8,128)S(1)}, u32[]{:S(2)}) copy-start(f32[1280,1024]{1,0:T(8,128)S(1)} %fusion.52) | copy-start | bytes 15728644
  379.7 257.6 %all-reduce.8.cloned.1.call-start = ((), (), s32[]{:S(2)}) async-start(), calls=%async_computation.5 | async-start | bytes 5242880 | tf_op jit(solution)/shard_map/psum | solution.py:162
  482.1 5.5 copy-start.5
  482.1 5.5 copy-start.6
  482.1 5.5 copy-start.27
  482.1 5.5 copy-start.30
  482.1 5.5 copy-start.37
  487.6 7.9 copy-start.18
  503.6 5.5 copy-start.10
  503.6 5.6 copy-start.11
  503.6 5.6 copy-start.21
  503.6 5.6 copy-start.35
  503.6 11.0 %slice-start = ((s8[7864320]{0:T(1024)(128)(4,1)}), s8[4194304]{0:T(1024)(128)(4,1)S(1)}, s32[]{:S(2)}) async-start(s8[7864320]{0:T(1024)(128)(4,1)} %bitcast.97), calls=%async_computation.8 | async-start | bytes 8388608
  509.2 5.4 slice-start.1
  528.2 5.8 copy-start.46
  534.0 157.3 %reduce-scatter.2.cloned.1.call-start = ((), (), s32[]{:S(2)}) async-start(), calls=%async_computation.2 | async-start | bytes 3276800 | tf_op jit(solution)/shard_map/reduce_scatter | solution.py:106
  545.2 7.3 copy-start.28
  545.2 7.3 copy-start.31
  545.2 7.3 copy-start.38
  545.2 7.3 copy-start.50
  545.2 254.5 %all-reduce.10.cloned.1.call-start = ((), (), s32[]{:S(2)}) async-start(), calls=%async_computation.7 | async-start | bytes 12582912 | tf_op jit(solution)/shard_map/psum | solution.py:171
  545.4 7.1 copy-start.52
  545.4 14.4 %slice-start.2 = ((s8[5242880]{0:T(1024)(128)(4,1)}), s8[4194304]{0:T(1024)(128)(4,1)S(1)}, s32[]{:S(2)}) async-start(s8[5242880]{0:T(1024)(128)(4,1)} %bitcast.99), calls=%async_computation.10 | async-start | bytes 8388608
  552.5 7.3 slice-start.3
  565.8 73.7 %copy-start.40 = (f32[1024]{0:T(1024)S(1)}, f32[1024]{0:T(1024)}, u32[]{:S(2)}) copy-start(f32[1024]{0:T(1024)} %param.18) | copy-start | bytes 12292
  639.5 7.3 copy-start.41
  639.5 7.2 copy-start.42
  639.5 7.2 copy-start.43
  639.5 7.2 copy-start.47
  799.7 5.8 copy-start.17
  801.9 6.0 copy-start.16
  (16 other events, 33.8 us)
Sparse Core Ops, SparseCore 0:
  9.6 57.5 all-gather.4
  112.2 182.0 all-gather.8
  295.9 52.9 all-gather.6
  379.8 102.2 all-reduce.5
  534.1 103.0 all-reduce.7
  640.0 51.2 reduce-scatter.1
  696.1 103.5 all-reduce.9
